TPU v7x, 32 devices: a whole 2x2x4 slice. The times are simulated.
32 devices in a mesh: ep: 16 (over z, x, core), dp: 2 (over y).
Axes of the slice: x: 2, y: 2, z: 4, core: 2. Of those that a mesh axis runs over, the one named last changes fastest.
Arguments:
- tokens: bfloat16 [256, 3584], P('ep'), may hold values from -6 to 6
- expert_ids: int32 [256, 8], P('ep'), may hold values from 0 to 15, all different within a row; in each aligned block of 16 rows (0 to 15, 16 to 31, ...) at most 16 rows name the same one
- route_logits: float32 [256, 8], P('ep'), may hold values from -8 to 8
- expert_gate: bfloat16 [16, 3584, 1024], P('ep', None, 'dp'), may hold values from -0.09375 to 0.09375
- expert_up: bfloat16 [16, 3584, 1024], P('ep', None, 'dp'), may hold values from -0.09375 to 0.09375
- expert_down: bfloat16 [16, 1024, 3584], P('ep', 'dp'), may hold values from -0.1875 to 0.1875
Outputs:
- mixed: bfloat16 [256, 3584], P(('ep', 'dp'))
Inputs may be any that keep to these rules, and one draw needn't show every extreme that they name: `expert_ids`: each row names 8 different experts of 0 to 15 and every expert is named by some row. Within the rows of one index of ep (aligned blocks of 16 rows) no expert is named more than 16 times, and some block names one expert exactly 16 times. Loads are heavy-tailed: a few experts take several times the mean.
All inputs are finite; a program needn't handle non-finite values.
Results may differ from a plain program's by a relative error of at most 0.015.
Values may be sent and summed in bfloat16 or wider, within the bound.
A program may use at most 64 MiB of HBM per device.

v0:
```python
import jax
import jax.numpy as jnp
from jax import lax
from jax.sharding import PartitionSpec as P

route_scale = 2.5


def on_device(tokens, expert_ids, route_logits, expert_gate, expert_up, expert_down):
    tok_rows, width = tokens.shape
    top = expert_ids.shape[1]
    n_ep = lax.axis_size("ep")
    n_dp = lax.axis_size("dp")
    experts = n_ep
    capacity = min(tok_rows, 4 * max(1, tok_rows * top // experts))
    flat_ids = expert_ids.reshape(-1).astype(jnp.int32)
    onehot = (flat_ids[:, None] == jnp.arange(experts, dtype=jnp.int32)[None, :]).astype(jnp.int32)
    earlier = jnp.cumsum(onehot, axis=0).astype(jnp.int32) - onehot
    within = jnp.sum(earlier * onehot, axis=1).astype(jnp.int32)
    slot_index = flat_ids * capacity + within
    token_of_slot = jnp.arange(tok_rows * top, dtype=jnp.int32) // top
    source_row = (
        jnp.full((experts * capacity,), tok_rows, jnp.int32).at[slot_index].set(token_of_slot)
    )
    extended = jnp.concatenate([tokens, jnp.zeros((1, width), tokens.dtype)], axis=0)
    outgoing = extended[source_row].reshape(n_ep, capacity, width)
    arrived = lax.all_to_all(outgoing, "ep", split_axis=0, concat_axis=0, tiled=True)
    received = arrived.reshape(n_ep * capacity, width)
    gate = jnp.dot(received, expert_gate[0], preferred_element_type=jnp.float32)
    upper = jnp.dot(received, expert_up[0], preferred_element_type=jnp.float32)
    hidden = (jax.nn.silu(gate) * upper).astype(jnp.bfloat16)
    partial_value = jnp.dot(hidden, expert_down[0], preferred_element_type=jnp.float32)
    partial_value = partial_value.reshape(n_ep, capacity, width)
    scores = jax.nn.sigmoid(route_logits)
    weights = route_scale * scores / jnp.sum(scores, axis=1, keepdims=True)
    member = lax.axis_index("dp")
    quarter = capacity // n_dp
    reduced = (
        lax.psum_scatter(partial_value.astype(jnp.bfloat16), "dp", scatter_dimension=1, tiled=True)
        .astype(jnp.float32)
        .astype(jnp.bfloat16)
    )
    back = lax.all_to_all(reduced, "ep", split_axis=0, concat_axis=0, tiled=True)
    offset = within - member * quarter
    held = ((offset >= 0) & (offset < quarter)).astype(jnp.float32)
    picked = flat_ids * quarter + jnp.clip(offset, 0, quarter - 1)
    values = back.reshape(experts * quarter, width)[picked].reshape(tok_rows, top, width)
    masked = weights * held.reshape(tok_rows, top)
    contrib = jnp.sum(masked[:, :, None] * values.astype(jnp.float32), axis=1)
    routed = lax.psum_scatter(
        contrib.astype(jnp.bfloat16), "dp", scatter_dimension=0, tiled=True
    ).astype(jnp.float32)
    return routed.astype(jnp.bfloat16)


def solution(mesh):
    placed = (
        P("ep", None),
        P("ep", None),
        P("ep", None),
        P("ep", None, "dp"),
        P("ep", None, "dp"),
        P("ep", "dp", None),
    )
    return jax.shard_map(
        on_device, mesh=mesh, in_specs=placed, out_specs=P(("ep", "dp"), None), check_vma=False
    )
```

profile of v0, /device:TPU:0, one launch (start us, length us, event | category | flops | bytes accessed | tf_op | source)
XLA Modules:
  0.0 147.7 jit_solution(4356112808054715986)
XLA Ops:
  6.5 0.0 reduce-scatter.7.cloned.1.call-start
  6.5 0.8 copy.15
  7.3 0.7 broadcast_multiply_fusion
  8.0 0.1 eq.15
  8.1 0.1 fusion.12
  8.2 0.2 reduce_window_sum.11
  8.3 0.2 select_reduce_fusion
  8.5 0.1 copy.17
  8.6 0.1 mul.67
  8.7 0.1 copy.18
  8.8 0.1 mul.71
  8.9 1.0 scatter_custom_fusion
  9.9 0.9 concatenate.3
  10.8 1.7 %gather_fusion = bf16[256,3584]{1,0:T(8,128)(2,1)S(1)} fusion(bf16[17,3584]{1,0:T(8,128)(2,1)S(1)} %concatenate.3, s32[1024]{0:T(1024)S(1)} %pad_clamp_fusion.1), kind=kCustom, calls=%fused_computation | custom fusion | bytes 3671040 | tf_op jit(solution)/shard_map/gather | solution.py:26
  12.5 0.0 copy-start.2
  12.5 50.5 %all_to_all.10 = bf16[16,16,3584]{2,1,0:T(8,128)(2,1)S(1)} all-to-all(bf16[16,16,3584]{2,1,0:T(8,128)(2,1)S(1)} %bitcast.54), channel_id=1, replica_groups=mesh['ep'=16,'dp'=2] {'ep'}, dimensions={0} | all-to-all | bytes 3670016 | tf_op jit(solution)/shard_map/all_to_all | solution.py:27
  63.0 0.0 copy-done.2
  63.0 0.0 copy-start.3
  63.0 1.1 fusion.3
  64.1 0.9 copy-done.3
  65.0 0.0 copy-start
  65.0 1.1 fusion.9
  66.2 0.9 copy-done
  67.1 1.1 fusion.20
  68.2 1.4 copy.21
  69.6 0.0 reduce-scatter.7.cloned.1.call-update
  69.6 28.4 %reduce-scatter.7.cloned.1.call-done = bf16[8,57344]{1,0:T(8,128)(2,1)} async-done(((bf16[16,57344]{1,0:T(8,128)(2,1)}), bf16[8,57344]{1,0:T(8,128)(2,1)}) %reduce-scatter.7.cloned.1.call-update) | async-done | bytes 917520
  98.0 1.4 copy.25
  99.5 0.0 copy-start.1
  99.5 1.4 copy.20
  100.9 5.6 %all-to-all-start.1 = ((bf16[16,8,3584]{2,1,0:T(8,128)(2,1)}), bf16[16,8,3584]{2,1,0:T(8,128)(2,1)S(1)}, u32[]{:S(2)}, u32[]{:S(2)}) async-start(bf16[16,8,3584]{2,1,0:T(8,128)(2,1)} %copy.20), calls=%async_computation.1 | async-start | bytes 1835008 | tf_op jit(solution)/shard_map/all_to_all | solution.py:43
  106.5 0.0 reduce-scatter.5.cloned.1.call-start
  106.6 0.1 and.14
  106.7 0.0 copy-done.1
  106.7 0.1 copy.16
  106.8 0.1 fusion.13
  106.9 0.1 divide_select_fusion
  107.0 20.1 %all-to-all-done.1 = bf16[16,8,3584]{2,1,0:T(8,128)(2,1)S(1)} async-done(((bf16[16,8,3584]{2,1,0:T(8,128)(2,1)}), bf16[16,8,3584]{2,1,0:T(8,128)(2,1)S(1)}, u32[]{:S(2)}, u32[]{:S(2)}) %all-to-all-start.1) | async-done | bytes 917536 | tf_op jit(solution)/shard_map/all_to_all | solution.py:43
  127.1 1.1 gather_fusion.1
  128.2 1.3 fusion.5
  129.5 0.0 reduce-scatter.5.cloned.1.call-update
  129.6 11.3 %reduce-scatter.5.cloned.1.call-done = bf16[8,3584]{1,0:T(8,128)(2,1)} async-done(((bf16[16,3584]{1,0:T(8,128)(2,1)}), bf16[8,3584]{1,0:T(8,128)(2,1)}) %reduce-scatter.5.cloned.1.call-update) | async-done | bytes 57360 | tf_op jit(solution)/shard_map/reduce_scatter | solution.py:50
  (6 shorter events, 0.0 us)
Async XLA Ops:
  6.5 91.5 %reduce-scatter.7.cloned.1.call-start = ((), (), s32[]{:S(2)}) async-start(), calls=%async_computation.5 | async-start | bytes 2752512
  12.5 50.5 %copy-start.2 = (bf16[1,3584,512]{2,1,0:T(8,128)(2,1)S(1)}, bf16[1,3584,512]{2,1,0:T(8,128)(2,1)}, u32[]{:S(2)}) copy-start(bf16[1,3584,512]{2,1,0:T(8,128)(2,1)} %param.9) | copy-start | bytes 11010052
  63.0 2.0 %copy-start.3 = (bf16[1,3584,512]{2,1,0:T(8,128)(2,1)S(1)}, bf16[1,3584,512]{2,1,0:T(8,128)(2,1)}, u32[]{:S(2)}) copy-start(bf16[1,3584,512]{2,1,0:T(8,128)(2,1)} %param.10) | copy-start | bytes 11010052
  65.0 2.0 %copy-start = (bf16[1,512,3584]{2,1,0:T(8,128)(2,1)S(1)}, bf16[1,512,3584]{2,1,0:T(8,128)(2,1)}, u32[]{:S(2)}) copy-start(bf16[1,512,3584]{2,1,0:T(8,128)(2,1)} %param.11) | copy-start | bytes 11010052
  99.5 7.2 %copy-start.1 = (f32[16,8]{0,1:T(8,128)S(1)}, f32[16,8]{0,1:T(8,128)}, u32[]{:S(2)}) copy-start(f32[16,8]{0,1:T(8,128)} %param.8) | copy-start | bytes 1540
  100.9 26.2 %all-to-all-start.1 = ((bf16[16,8,3584]{2,1,0:T(8,128)(2,1)}), bf16[16,8,3584]{2,1,0:T(8,128)(2,1)S(1)}, u32[]{:S(2)}, u32[]{:S(2)}) async-start(bf16[16,8,3584]{2,1,0:T(8,128)(2,1)} %copy.20), calls=%async_computation.1 | async-start | bytes 1835008 | tf_op jit(solution)/shard_map/all_to_all | solution.py:43
  106.5 34.3 %reduce-scatter.5.cloned.1.call-start = ((), (), s32[]{:S(2)}) async-start(), calls=%async_computation.4 | async-start | bytes 172032 | tf_op jit(solution)/shard_map/reduce_scatter | solution.py:50
Sparse Core Ops, SparseCore 0:
  69.7 28.2 reduce-scatter.6
  129.7 11.0 reduce-scatter.4
where the time goes:
time: 148 us
  waiting for transfers between devices  59.8 us (40%)
  blocking collectives  50.5 us (34%)
  between operations  13.6 us (9%)
  local copies, waits for them, and re-layouts  12.2 us (8%)
  starting transfers between devices  5.66 us (4%)
  matrix products  3.34 us (2%)
  other arithmetic  2.68 us (2%)
    all_to_all x1, blocking collectives, on_device(): lax.all_to_all(outgoing, 'ep', split_axis=0, concat_axis=0, tiled=True)  50.5 us
    unnamed x3, waiting for transfers between devices  28.4 us
    all_to_all x1, waiting for transfers between devices, on_device(): lax.all_to_all(reduced, 'ep', split_axis=0, concat_axis=0, tiled=True)  20.1 us
    reduce_scatter x1, waiting for transfers between devices, on_device(): lax.psum_scatter(contrib.astype(jnp.bfloat16), 'dp', scatter_dimension=0,...  11.3 us
    unnamed x13, local copies, waits for them, and re-layouts  6.93 us
    all_to_all x1, starting transfers between devices, on_device(): lax.all_to_all(reduced, 'ep', split_axis=0, concat_axis=0, tiled=True)  5.62 us
  transfers between devices with their start and end apart: 3, of which 3 were waited for; matrix products, arithmetic and copies ran while one was open for 0% of the time, Pallas kernels for 0%

commit v1 on v0

--- a/solution.py
+++ b/solution.py
@@ -1,12 +1,16 @@
+import functools
+
 import jax
 import jax.numpy as jnp
 from jax import lax
+from jax.experimental import pallas as pl
+from jax.experimental.pallas import tpu as pltpu
 from jax.sharding import PartitionSpec as P
 
 route_scale = 2.5
 
 
-def on_device(tokens, expert_ids, route_logits, expert_gate, expert_up, expert_down):
+def by_slots(tokens, expert_ids, route_logits, expert_gate, expert_up, expert_down):
     tok_rows, width = tokens.shape
     top = expert_ids.shape[1]
     n_ep = lax.axis_size("ep")
@@ -53,6 +57,342 @@
     return routed.astype(jnp.bfloat16)
 
 
+MESH = pl.DeviceIdType.MESH
+LANES = 128
+RIGHT, LEFT, ACROSS, SIDE, CORE = range(5)
+
+
+def exchange_kernel(
+    planes, tokens_ref, ids_ref, logits_ref, gate_hbm, up_hbm, down_hbm, out_ref,
+    tok, w_gate, w_up, w_down, hid, wcol, theirs, part, from_core, from_first, line_out, line_in,
+    last_out, last_in,
+    weight_sem, tok_send, tok_recv, core_send, core_recv, first_send, first_recv,
+    line_send, line_recv, last_send, last_recv,
+):
+    rows, width = tokens_ref.shape
+    top = ids_ref.shape[1]
+    hidden = gate_hbm.shape[2]
+    wide = tok.shape[1]
+    half = wide // 2
+    sub = rows // 2
+    me, y = lax.axis_index("ep"), lax.axis_index("dp")
+    c, x, z = me % 2, (me // 2) % 2, me // 4
+
+    def ep_of(zz, xx, cc):
+        return (zz * 2 + xx) * 2 + cc
+
+    def device(kind):
+        if kind == RIGHT:
+            return (ep_of(z + 1, x, c), y)
+        if kind == LEFT:
+            return (ep_of(z - 1, x, c), y)
+        if kind == ACROSS:
+            return (ep_of(z, 1 - x, c), y)
+        if kind == SIDE:
+            return (me, 1 - y)
+        return (ep_of(z, x, 1 - c), y)
+
+    loads = [
+        pltpu.make_async_copy(src.at[0], dst, weight_sem.at[i])
+        for i, (src, dst) in enumerate(((gate_hbm, w_gate), (up_hbm, w_up), (down_hbm, w_down)))
+    ]
+    for load in loads:
+        load.start()
+
+    barrier = pltpu.get_barrier_semaphore()
+
+    def greet(kind):
+        pl.semaphore_signal(barrier, inc=1, device_id=device(kind), device_id_type=MESH)
+
+    for kind in (ACROSS, SIDE, CORE):
+        greet(kind)
+    pl.when(z > 0)(lambda: greet(LEFT))
+    pl.when(z < planes - 1)(lambda: greet(RIGHT))
+
+    scores = jax.nn.sigmoid(logits_ref[...])
+    weights = route_scale * scores / jnp.sum(scores, axis=1, keepdims=True)
+    lane = lax.broadcasted_iota(jnp.int32, (rows, LANES), 1)
+    dense = jnp.zeros((rows, LANES), jnp.float32)
+    for k in range(top):
+        dense = dense + jnp.where(lane == ids_ref[:, k : k + 1], weights[:, k : k + 1], 0.0)
+    coarse = dense.astype(jnp.bfloat16)
+    fine = (dense - coarse.astype(jnp.float32)).astype(jnp.bfloat16)
+    own_rows = pl.ds(pl.multiple_of(me * rows, rows), rows)
+    tok[own_rows, :width] = tokens_ref[...]
+    tok[own_rows, width : width + LANES] = coarse
+    tok[own_rows, width + LANES :] = fine
+
+    middle = jnp.where(z > 0, 1, 0) + jnp.where(z < planes - 1, 1, 0)
+    pl.semaphore_wait(barrier, 3 + middle)
+
+    def unit(block, h):
+        return tok.at[
+            pl.ds(pl.multiple_of(block * rows, rows), rows),
+            pl.ds(pl.multiple_of(h * half, LANES), half),
+        ]
+
+    def token_copy(kind, block, h):
+        return pltpu.make_async_remote_copy(
+            src_ref=unit(block, h),
+            dst_ref=unit(block, h),
+            send_sem=tok_send.at[kind, block, h],
+            recv_sem=tok_recv.at[block, h],
+            device_id=device(kind),
+            device_id_type=MESH,
+        )
+
+    def on_line(do, arrived, d, k):
+        h = y if k == 0 else 1 - y
+
+        def pass_on(block, right, left):
+            if arrived:
+                token_copy(CORE, block, h).wait_recv()
+            if right:
+                pl.when(z < planes - 1)(lambda: do(token_copy(RIGHT, block, h)))
+            if left:
+                pl.when(z > 0)(lambda: do(token_copy(LEFT, block, h)))
+            if k == 0:
+                do(token_copy(ACROSS, block, h))
+            do(token_copy(CORE, block, h))
+
+        if d == 0:
+            pass_on(me, True, True)
+        else:
+            pl.when(z - d >= 0)(lambda: pass_on(ep_of(z - d, x, c), True, False))
+            pl.when(z + d < planes)(lambda: pass_on(ep_of(z + d, x, c), False, True))
+
+    def at_distance(d, act):
+        if d == 0:
+            act(z)
+        else:
+            pl.when(z - d >= 0)(lambda: act(z - d))
+            pl.when(z + d < planes)(lambda: act(z + d))
+
+    def token_moves(do, arrived):
+        for step in range(planes + 2):
+            if step < planes:
+                for k in range(2):
+                    on_line(do, arrived and step > 0, step, k)
+            if 0 <= step - 1 < planes:
+
+                def crossed(zz):
+                    block = ep_of(zz, 1 - x, c)
+                    if arrived:
+                        token_copy(CORE, block, y).wait_recv()
+                    do(token_copy(SIDE, block, y))
+                    do(token_copy(CORE, block, y))
+
+                at_distance(step - 1, crossed)
+            if 0 <= step - 2 < planes:
+
+                def sided(zz):
+                    block = ep_of(zz, 1 - x, c)
+                    if arrived:
+                        token_copy(CORE, block, 1 - y).wait_recv()
+                    do(token_copy(CORE, block, 1 - y))
+
+                at_distance(step - 2, sided)
+
+    token_moves(lambda copy: copy.start(), True)
+    for zz in range(planes):
+        for xx in range(2):
+            for h in range(2):
+                token_copy(CORE, ep_of(zz, xx, 1 - c), h).wait_recv()
+
+    loads[0].wait()
+    loads[1].wait()
+    step_f = 256
+
+    def project(i, carry):
+        cols = pl.ds(pl.multiple_of(i * step_f, step_f), step_f)
+        gate = jnp.dot(tok[:, :width], w_gate[:, cols], preferred_element_type=jnp.float32)
+        upper = jnp.dot(tok[:, :width], w_up[:, cols], preferred_element_type=jnp.float32)
+        value = (gate / (1.0 + jnp.exp(-gate)) * upper).astype(jnp.bfloat16)
+        value = value.reshape(planes * 2, 2, rows, step_f)
+        for cc in range(2):
+            hid[cc, :, cols] = value[:, cc].reshape(planes * 2 * rows, step_f)
+        return carry
+
+    lax.fori_loop(0, hidden // step_f, project, 0)
+
+    table = tok[:, width : width + LANES].astype(jnp.float32) + tok[:, width + LANES :].astype(
+        jnp.float32
+    )
+    every = lax.broadcasted_iota(jnp.int32, table.shape, 1)
+    chosen = jnp.sum(jnp.where(every == me, table, 0.0), axis=1, keepdims=True)
+    chosen = jnp.broadcast_to(chosen, table.shape).reshape(planes * 2, 2, rows, LANES)
+    for cc in range(2):
+        wcol[cc] = chosen[:, cc].reshape(planes * 2 * rows, LANES)
+
+    loads[2].wait()
+    step_n = 512
+
+    def expand(cc, dst):
+        def one(i, carry):
+            cols = pl.ds(pl.multiple_of(i * step_n, step_n), step_n)
+            value = jnp.dot(hid[cc], w_down[:, cols], preferred_element_type=jnp.float32)
+            value = value * wcol[cc][:, :1]
+            for zz in range(planes):
+                for xx in range(2):
+                    for yy in range(2):
+                        first = jnp.where(cc == 0, yy, xx)
+                        second = jnp.where(cc == 0, xx, yy)
+                        at = ((zz * 2 + xx) * 2 + yy) * sub
+                        dst[zz, first, second, :, cols] = value[at : at + sub].astype(jnp.bfloat16)
+            return carry
+
+        lax.fori_loop(0, width // step_n, one, 0)
+
+    def core_copy(t):
+        return pltpu.make_async_remote_copy(
+            src_ref=theirs.at[t], dst_ref=from_core.at[t],
+            send_sem=core_send.at[t], recv_sem=core_recv.at[t],
+            device_id=device(CORE), device_id_type=MESH,
+        )
+
+    expand(1 - c, theirs)
+    for d in range(planes - 1, -1, -1):
+        at_distance(d, lambda t: core_copy(t).start())
+    expand(c, part)
+
+    a = jnp.where(c == 0, y, x)
+    b = jnp.where(c == 0, x, y)
+    swap_y = (me, 1 - y)
+    swap_x = (ep_of(z, 1 - x, c), y)
+    first_device = tuple(jnp.where(c == 0, p, q) for p, q in zip(swap_y, swap_x))
+    last_device = tuple(jnp.where(c == 0, q, p) for p, q in zip(swap_y, swap_x))
+
+    def first_copy(t):
+        return pltpu.make_async_remote_copy(
+            src_ref=part.at[t, 1 - a], dst_ref=from_first.at[t],
+            send_sem=first_send.at[t], recv_sem=first_recv.at[t],
+            device_id=first_device, device_id_type=MESH,
+        )
+
+    def add_core(t):
+        core_copy(t).wait_recv()
+        part[t] = (part[t].astype(jnp.float32) + from_core[t].astype(jnp.float32)).astype(
+            jnp.bfloat16
+        )
+        first_copy(t).start()
+
+    for d in range(planes - 1, -1, -1):
+        at_distance(d, add_core)
+
+    def line_copy(side, t):
+        return pltpu.make_async_remote_copy(
+            src_ref=line_out.at[t], dst_ref=line_in.at[side, t],
+            send_sem=line_send.at[t], recv_sem=line_recv.at[side, t],
+            device_id=device(RIGHT if side == 0 else LEFT), device_id_type=MESH,
+        )
+
+    def kept(t):
+        first_copy(t).wait_recv()
+        return part[t, a].astype(jnp.float32) + from_first[t].astype(jnp.float32)
+
+    def relay(side, t):
+        line_out[t] = kept(t).astype(jnp.bfloat16)
+        inner = z > 0 if side == 0 else z < planes - 1
+
+        @pl.when(inner)
+        def _():
+            line_copy(side, t).wait_recv()
+            line_out[t] = (
+                line_out[t].astype(jnp.float32) + line_in[side, t].astype(jnp.float32)
+            ).astype(jnp.bfloat16)
+
+        line_copy(side, t).start()
+
+    for d in range(planes - 1, 0, -1):
+        pl.when(z + d < planes)(lambda: relay(0, z + d))
+        pl.when(z - d >= 0)(lambda: relay(1, z - d))
+
+    last_out[...] = kept(z)
+
+    def gathered(side):
+        line_copy(side, z).wait_recv()
+        last_out[...] = last_out[...] + line_in[side, z].astype(jnp.float32)
+
+    pl.when(z > 0)(lambda: gathered(0))
+    pl.when(z < planes - 1)(lambda: gathered(1))
+    line_out[z] = last_out[...].astype(jnp.bfloat16)
+    final = pltpu.make_async_remote_copy(
+        src_ref=line_out.at[z, 1 - b], dst_ref=last_in,
+        send_sem=last_send, recv_sem=last_recv,
+        device_id=last_device, device_id_type=MESH,
+    )
+    final.start()
+    final.wait_recv()
+    out_ref[...] = (last_out[b] + last_in[...].astype(jnp.float32)).astype(out_ref.dtype)
+
+    final.wait_send()
+    token_moves(lambda copy: copy.wait_send(), False)
+    for t in range(planes):
+        core_copy(t).wait_send()
+        first_copy(t).wait_send()
+    for d in range(1, planes):
+        pl.when(z + d < planes)(lambda: line_copy(0, z + d).wait_send())
+        pl.when(z - d >= 0)(lambda: line_copy(1, z - d).wait_send())
+
+
+def by_gather(tokens, expert_ids, route_logits, expert_gate, expert_up, expert_down):
+    rows, width = tokens.shape
+    hidden = expert_gate.shape[2]
+    n_ep, n_dp = lax.axis_size("ep"), lax.axis_size("dp")
+    planes = n_ep // 4
+    wide = width + 2 * LANES
+    sub = rows // n_dp
+    vmem = pl.BlockSpec(memory_space=pltpu.VMEM)
+    anywhere = pl.BlockSpec(memory_space=pl.ANY)
+    bf16, f32, dma = jnp.bfloat16, jnp.float32, pltpu.SemaphoreType.DMA
+    return pl.pallas_call(
+        functools.partial(exchange_kernel, planes),
+        out_shape=jax.ShapeDtypeStruct((sub, width), bf16),
+        in_specs=[vmem, vmem, vmem, anywhere, anywhere, anywhere],
+        out_specs=vmem,
+        scratch_shapes=[
+            pltpu.VMEM((n_ep * rows, wide), bf16),
+            pltpu.VMEM((width, hidden), bf16),
+            pltpu.VMEM((width, hidden), bf16),
+            pltpu.VMEM((hidden, width), bf16),
+            pltpu.VMEM((2, n_ep * rows // 2, hidden), bf16),
+            pltpu.VMEM((2, n_ep * rows // 2, LANES), f32),
+            pltpu.VMEM((planes, 2, 2, sub, width), bf16),
+            pltpu.VMEM((planes, 2, 2, sub, width), bf16),
+            pltpu.VMEM((planes, 2, 2, sub, width), bf16),
+            pltpu.VMEM((planes, 2, sub, width), bf16),
+            pltpu.VMEM((planes, 2, sub, width), bf16),
+            pltpu.VMEM((2, planes, 2, sub, width), bf16),
+            pltpu.VMEM((2, sub, width), f32),
+            pltpu.VMEM((sub, width), bf16),
+            dma((3,)),
+            dma((5, n_ep, 2)),
+            dma((n_ep, 2)),
+            dma((planes,)),
+            dma((planes,)),
+            dma((planes,)),
+            dma((planes,)),
+            dma((planes,)),
+            dma((2, planes)),
+            dma,
+            dma,
+        ],
+        compiler_params=pltpu.CompilerParams(
+            collective_id=0, has_side_effects=True, vmem_limit_bytes=56 * 1024 * 1024
+        ),
+    )(tokens, expert_ids, route_logits, expert_gate, expert_up, expert_down)
+
+
+def on_device(tokens, expert_ids, route_logits, expert_gate, expert_up, expert_down):
+    rows, width = tokens.shape
+    n_ep, n_dp = lax.axis_size("ep"), lax.axis_size("dp")
+    crowded = 4 * max(1, rows * expert_ids.shape[1] // n_ep) >= rows
+    fits = n_dp == 2 and n_ep % 4 == 0 and n_ep <= LANES and rows == 16 and width % 512 == 0
+    fits = fits and expert_gate.shape[0] == 1 and expert_gate.shape[2] % 256 == 0
+    run = by_gather if crowded and fits else by_slots
+    return run(tokens, expert_ids, route_logits, expert_gate, expert_up, expert_down)
+
+
 def solution(mesh):
     placed = (
         P("ep", None),

time: 148 us -> 54.5 us (0.37)
  waiting for transfers between devices: 59.8 us -> 0 us
  blocking collectives: 50.5 us -> 0 us
  Pallas kernels: 0 us -> 50.1 us
  between operations: 13.6 us -> 0.01 us
  local copies, waits for them, and re-layouts: 12.2 us -> 4.15 us
  starting transfers between devices: 5.66 us -> 0 us
  matrix products: 3.34 us -> 0 us
  other arithmetic: 2.68 us -> 0 us
    all_to_all x1 -> x0, blocking collectives: 50.5 us -> none  [on_device(): lax.all_to_all(outgoing, 'ep', split_axis=0, concat_axis=0, tiled=True)]
    pallas_call x0 -> x1, Pallas kernels: none -> 50.1 us  [by_gather(): pl.pallas_call(functools.partial(exchange_kernel, planes), out_shape=jax....]
    unnamed x3 -> x0, waiting for transfers between devices: 28.4 us -> none
    all_to_all x1 -> x0, waiting for transfers between devices: 20.1 us -> none  [on_device(): lax.all_to_all(reduced, 'ep', split_axis=0, concat_axis=0, tiled=True)]
    reduce_scatter x1 -> x0, waiting for transfers between devices: 11.3 us -> none  [on_device(): lax.psum_scatter(contrib.astype(jnp.bfloat16), 'dp', scatter_dimension=0,...]
    all_to_all x1 -> x0, starting transfers between devices: 5.62 us -> none  [on_device(): lax.all_to_all(reduced, 'ep', split_axis=0, concat_axis=0, tiled=True)]
    dot_general x3 -> x0, matrix products: 3.34 us -> none  [the longest x1 1.13 us: on_device(): upper = jnp.dot(received, expert_up[0], preferred_element_type=jnp.float32)]
    gather x2 -> x0, local copies, waits for them, and re-layouts: 2.83 us -> none  [the longest x1 1.72 us: on_device(): outgoing = extended[source_row].reshape(n_ep, capacity, width)]
  transfers between devices with their start and end apart: 3 -> 0, of which waited for: 3 -> 0; matrix products, arithmetic and copies ran while one was open for 0% -> 0% of each run, Pallas kernels for 0% -> 0%
where the time goes in v1:
time: 54.5 us; the launch traced here: 54.3 us
  Pallas kernels  50.1 us (92%)
  local copies, waits for them, and re-layouts  4.15 us (8%)
    pallas_call x1, Pallas kernels, by_gather(): pl.pallas_call(functools.partial(exchange_kernel, planes), out_shape=jax....  50.1 us
    unnamed x3, local copies, waits for them, and re-layouts  4.15 us

profile of v1, /device:TPU:0, one launch (start us, length us, event | category | flops | bytes accessed | tf_op | source)
XLA Modules:
  0.0 54.3 jit_solution(8411185208830586875)
XLA Ops:
  0.0 1.4 %copy.7.ids_ref = s32[16,8]{1,0:T(8,128)} copy(s32[16,8]{0,1:T(8,128)} %param.7) | data formatting | bytes 1024 | tf_op args[1]
  1.4 1.3 %copy.8.logits_ref = f32[16,8]{1,0:T(8,128)} copy(f32[16,8]{0,1:T(8,128)} %param.8) | data formatting | bytes 1024 | tf_op args[2]
  2.7 50.1 %shard_map.64 = bf16[8,3584]{1,0:T(8,128)(2,1)} custom-call(bf16[16,3584]{1,0:T(8,128)(2,1)} %tokens_ref.1, s32[16,8]{1,0:T(8,128)} %copy.7.ids_ref, f32[16,8]{1,0:T(8,128)} %copy.8.logits_ref, bf16[1,3584,512]{2,1,0:T(8,128)(2,1)} %gate_hbm.1, bf16[1,3584,512]{2,1,0:T(8,128)(2,1)} %up_hbm.1, bf16[1,512,3584]{2,1,0:T(8,128)(2,1)} %down_hbm.1), custom_call_target="tpu_custom_call" | custom-call | tf_op jit(solution)/shard_map/pallas_call | solution.py:348
  52.8 1.4 %copy.10 = bf16[8,3584]{1,0:T(8,128)(2,1)} copy(bf16[8,3584]{1,0:T(8,128)(2,1)} %shard_map.64) | data formatting | bytes 114688
